TPU v7x, 32 devices: a whole 2x2x4 slice. The times are simulated.
32 devices in a mesh: groups: 2 (over y), gx: 4 (over z), gy: 4 (over x, core).
Axes of the slice: x: 2, y: 2, z: 4, core: 2. Of those that a mesh axis runs over, the one named last changes fastest.
Arguments:
- tokens: bfloat16 [2, 16, 16384], P(None, 'groups', 'gx'), parts along dimension 1, may hold values from -20 to 20, as said below
- lengths: int32 [2, 16], P(None, ('groups', 'gx')), parts along dimension 1, may hold values from 1 to 1024, as said below
- norm_gain: bfloat16 [16384], P('gx'), may hold values from 0.5 to 2
- w_query: bfloat16 [16384, 8192], P('gx', 'gy'), may hold values from -1.171875 to 1.171875
- key_value_weight: bfloat16 [16384, 4, 256], P('gx', 'gy'), may hold values from -0.046875 to 0.046875
- w_out: bfloat16 [8192, 16384], P('gy', 'gx'), may hold values from -0.0625 to 0.0625
- cache: bfloat16 [2, 16, 1024, 4, 2, 128], P(None, ('groups', 'gx'), None, 'gy'), parts along dimension 1, may hold values from -16 to 16
Outputs:
- layer_out: bfloat16 [2, 16, 16384], P(None, 'groups', 'gx'), parts along dimension 1
There are 2 independent parts, one for each index of `groups`. A program takes and returns all parts, laid end to end along the dimension named above; an argument that names none is the same for every part. Nothing has to cross between parts.
Inputs may be any that keep to these rules, and one draw needn't show every extreme that they name: `tokens`: entries vary with the feature and the row. `lengths`: some rollout has exactly 1024 cached positions in every draw.
All inputs are finite; a program needn't handle non-finite values.
Results may differ from a plain program's by a relative error of at most 0.012.
The roundings to bfloat16 on the way count: a program that leaves them out, or rounds other values in their place, can miss the bound.
Values may be sent and summed in bfloat16 or wider, within the bound.
No kernel may reach another device: no remote copies, remote signals or barrier semaphores. Data moves between devices by JAX's collectives and lax.ppermute only.
A program may use at most 128 MiB of HBM per device.

v0:
```python
import jax
import jax.numpy as jnp
from jax import lax
from jax.sharding import PartitionSpec as P

MODEL_WIDTH = 16384
HEAD_SIZE = 128


def rotate(vectors, positions):
    half = vectors.shape[-1] // 2
    freq = 500000.0 ** (-2.0 * jnp.arange(half, dtype=jnp.float32) / vectors.shape[-1])
    angle = positions[..., None] * freq
    cosine = jnp.cos(angle)
    sine = jnp.sin(angle)
    first = vectors[..., :half]
    second = vectors[..., half:]
    return jnp.concatenate(
        [first * cosine - second * sine, second * cosine + first * sine], axis=-1
    )


def attend(query_sum, keyval_sum, local_squares, lengths, cache):
    batches, rows_here = lengths.shape
    score_scale = lax.rsqrt(local_squares / MODEL_WIDTH + 1e-05)
    heads_kv = keyval_sum.shape[2]
    query_group = query_sum.shape[2] // (heads_kv * HEAD_SIZE)
    query = (
        query_sum.reshape(batches, rows_here, heads_kv, query_group, HEAD_SIZE)
        * score_scale[:, :, None, None, None]
    )
    key_value = keyval_sum * score_scale[:, :, None, None]
    positions = lengths.astype(jnp.float32)
    rotated_query = rotate(query, positions[:, :, None, None]).astype(jnp.bfloat16)
    rkey = rotate(key_value[..., :HEAD_SIZE], positions[:, :, None])
    value_new = key_value[..., HEAD_SIZE:]
    inv_root = 1.0 / jnp.sqrt(jnp.float32(HEAD_SIZE))
    keys = cache[:, :, :, :, 0, :]
    values = cache[:, :, :, :, 1, :]
    scores = (
        jnp.einsum("mrkgd,mrskd->mrkgs", rotated_query, keys, preferred_element_type=jnp.float32)
        * inv_root
    )
    valid = jnp.arange(cache.shape[2], dtype=jnp.int32)[None, None, :] < lengths[:, :, None]
    scores = jnp.where(valid[:, :, None, None, :], scores, -1e30)
    new_score = (
        jnp.sum(rotated_query.astype(jnp.float32) * rkey[:, :, :, None, :], axis=-1) * inv_root
    )
    top = jnp.maximum(jnp.max(scores, axis=-1), new_score)
    weights = jnp.exp(scores - top[..., None])
    new_weight = jnp.exp(new_score - top)
    total = jnp.sum(weights, axis=-1) + new_weight
    summed = jnp.einsum(
        "mrkgs,mrskd->mrkgd",
        weights.astype(jnp.bfloat16),
        values,
        preferred_element_type=jnp.float32,
    )
    summed = summed + new_weight[..., None] * value_new[:, :, :, None, :]
    return (
        (summed / total[..., None])
        .astype(jnp.bfloat16)
        .reshape(batches, rows_here, heads_kv * query_group * HEAD_SIZE)
    )


def local(tokens, lengths, norm_gain, w_query, key_value_weight, w_out, cache):
    x_full = tokens.astype(jnp.float32)
    squares = jnp.sum(x_full * x_full, axis=-1)
    normed = (x_full * norm_gain.astype(jnp.float32)).astype(jnp.bfloat16)
    query_part = jnp.einsum("mrd,dc->mrc", normed, w_query, preferred_element_type=jnp.float32)
    keyval_part = jnp.einsum(
        "mrd,dkc->mrkc", normed, key_value_weight, preferred_element_type=jnp.float32
    )
    query_sum, keyval_sum, local_squares = (
        lax.psum_scatter(query_part, "gx", scatter_dimension=1, tiled=True),
        lax.psum_scatter(keyval_part, "gx", scatter_dimension=1, tiled=True),
        lax.psum_scatter(squares, "gx", scatter_dimension=1, tiled=True),
    )
    attended = attend(query_sum, keyval_sum, local_squares, lengths, cache)
    projected = jnp.einsum(
        "mrc,cd->mrd",
        lax.all_gather(attended, "gx", axis=1, tiled=True),
        w_out,
        preferred_element_type=jnp.float32,
    )
    summed_heads = lax.psum(projected, "gy")
    return (x_full + summed_heads).astype(jnp.bfloat16)


def solution(mesh):
    placed = (
        P(None, "groups", "gx"),
        P(None, ("groups", "gx")),
        P("gx"),
        P("gx", "gy"),
        P("gx", "gy", None),
        P("gy", "gx"),
        P(None, ("groups", "gx"), None, "gy", None, None),
    )
    return jax.shard_map(
        local, mesh=mesh, in_specs=placed, out_specs=P(None, "groups", "gx"), check_vma=False
    )
```

profile of v0, /device:TPU:0, one launch (start us, length us, event | category | flops | bytes accessed | tf_op | source)
XLA Modules:
  0.0 122.0 jit_solution(11372717634072038642)
XLA Ops:
  6.5 0.8 convert_element_type.46
  7.4 8.8 %fusion.2 = f32[2,8,2048]{2,1,0:T(8,128)} fusion(bf16[4096,2048]{1,0:T(8,128)(2,1)} %param.10, bf16[2,8,4096]{2,1,0:T(8,128)(2,1)} %param.7, f32[4096]{0:T(1024)S(1)} %convert_element_type.46), kind=kOutput, calls=%fused_computation.2 | convolution fusion | flops 268632064 | bytes 17055744 | tf_op jit(solution)/shard_map/mrd,dc->mrc/dot_general | solution.py:71
  16.3 0.1 fusion.13
  16.4 0.1 iota_compare_fusion
  16.5 0.4 fusion.9
  16.9 0.7 dynamic-slice
  18.3 0.1 multiply_cosine_fusion.1
  18.4 20.8 %all-reduce.3 = (f32[2,8]{1,0:T(2,128)S(1)}, f32[2,8,1,256]{3,1,0,2:T(8,128)S(1)}) all-reduce(f32[2,8]{1,0:T(2,128)S(1)} %fusion.13, f32[2,8,1,256]{3,1,0,2:T(8,128)S(1)} %fusion.9), channel_id=3, replica_groups=mesh['groups'=2,'gx'=4,'gy'=4] {'gx'}, use_global_device_ids=true, to_apply=%region_2.0.clone | all-reduce | flops 4112 | bytes 32896
  39.2 0.1 fusion.32
  39.3 0.1 dynamic-slice_multiply_fusion
  39.4 0.1 fusion.29
  39.5 6.9 %fusion.35 = (bf16[2,2,1024,1,1,128]{5,4,3,2,1,0:T(2,128)(2,1)}, bf16[2,2,1024,1,1,128]{5,4,3,2,1,0:T(2,128)(2,1)}) fusion(bf16[2,2,1024,1,2,128]{5,4,3,2,1,0:T(2,128)(2,1)} %param.13), kind=kLoop, calls=%fused_computation.55 | loop fusion | bytes 4194304 | tf_op jit(solution)/shard_map/slice | solution.py:38
  46.4 0.1 maximum_bitcast_fusion
  46.5 7.3 %all-reduce.9.cloned.1.call-done = f32[2,8,2048]{2,1,0:T(8,128)} async-done(((f32[2,8,2048]{2,1,0:T(8,128)}), f32[2,8,2048]{2,1,0:T(8,128)}) %all-reduce.9.cloned.1.call-update) | async-done | bytes 131088
  53.9 0.9 constant_dynamic-slice_fusion
  54.9 0.1 subtract_convert_fusion
  55.0 0.2 multiply_reduce_fusion
  55.1 2.1 %fusion.36 = (f32[2,2,16]{2,1,0:T(2,128)S(1)}, f32[2,2,16,1024]{3,2,1,0:T(8,128)S(1)}) fusion(bf16[2,2,1024,1,1,128]{5,4,3,2,1,0:T(2,128)(2,1)} %get-tuple-element.9, bf16[2,2,16,64]{3,2,1,0:T(8,128)(2,1)S(1)} %bitcast.38, bf16[2,2,16,64]{3,2,1,0:T(8,128)(2,1)S(1)} %bitcast.37, pred[2,2,1024]{2,1,0:T(4,128)(4,1)S(1)} %iota_compare_fusion), kind=kOutput, calls=%fused_computation.56 | convolution fusion | flops 17006528 | bytes 1331456 | tf_op jit(solution)/shard_map/mrkgd,mrskd->mrkgs/dot_general | solution.py:41
  57.3 0.2 fusion.15
  57.5 1.9 %fusion.8 = bf16[2,2,16,128]{3,2,1,0:T(8,128)(2,1)S(1)} fusion(bf16[2,2,1024,1,1,128]{5,4,3,2,1,0:T(2,128)(2,1)} %get-tuple-element.10, f32[2,2,16,1024]{3,2,1,0:T(8,128)S(1)} %get-tuple-element.18, f32[2,2,16]{2,1,0:T(2,128)S(1)} %multiply_maximum_fusion, f32[2,2,16]{2,1,0:T(2,128)S(1)} %get-tuple-element.7, f32[2,2,128]{2,1,0:T(2,128)S(1)} %slice_bitcast_fusion, ...), kind=kOutput, calls=%fused_computation.10 | convolution fusion | flops 16941056 | bytes 1329920 | tf_op jit(solution)/shard_map/mrkgs,mrskd->mrkgd/dot_general | solution.py:53
  59.4 13.1 %all_gather.3 = bf16[2,8,2048]{2,0,1:T(2,128)(2,1)S(1)} all-gather(bf16[2,2,2048]{2,0,1:T(2,128)(2,1)S(1)} %copy.12), channel_id=1, replica_groups=mesh['groups'=2,'gx'=4,'gy'=4] {'gx'}, dimensions={1}, use_global_device_ids=true | all-gather | bytes 81920 | tf_op jit(solution)/shard_map/all_gather | solution.py:83
  72.6 8.8 %fusion = f32[2,8,4096]{2,1,0:T(8,128)} fusion(bf16[2048,4096]{1,0:T(8,128)(2,1)} %param.12, bf16[2,8,2048]{2,0,1:T(2,128)(2,1)S(1)} %all_gather.3), kind=kOutput, calls=%fused_computation | convolution fusion | flops 268435456 | bytes 17104896 | tf_op jit(solution)/shard_map/mrc,cd->mrd/dot_general | solution.py:81
  81.3 32.2 %all-reduce.7.cloned.1.call-done = f32[2,8,4096]{2,1,0:T(8,128)} async-done(((f32[2,8,4096]{2,1,0:T(8,128)}), f32[2,8,4096]{2,1,0:T(8,128)}) %all-reduce.7.cloned.1.call-update) | async-done | bytes 262160 | tf_op jit(solution)/shard_map/psum | solution.py:87
  113.5 1.6 %fusion.14 = bf16[2,8,4096]{2,1,0:T(8,128)(2,1)} fusion(f32[2,8,4096]{2,1,0:T(8,128)} %all-reduce.7.cloned.1.call-done, bf16[2,8,4096]{2,1,0:T(8,128)(2,1)S(1)} %copy-done.1), kind=kLoop, calls=%fused_computation.19 | loop fusion | flops 196608 | bytes 524288 | tf_op jit(solution)/shard_map/convert_element_type | solution.py:88
  (21 shorter events, 0.3 us)
Async XLA Ops:
  6.5 10.0 %copy-start = (bf16[4096,1,256]{2,0,1:T(8,128)(2,1)S(1)}, bf16[4096,1,256]{2,0,1:T(8,128)(2,1)}, u32[]{:S(2)}) copy-start(bf16[4096,1,256]{2,0,1:T(8,128)(2,1)} %param.11) | copy-start | bytes 6291460
  6.5 47.3 %all-reduce.9.cloned.1.call-start = ((), (), s32[]{:S(2)}) async-start(), calls=%async_computation.1 | async-start | bytes 262144
  7.4 8.9 %copy-start.1 = (bf16[2,8,4096]{2,1,0:T(8,128)(2,1)S(1)}, bf16[2,8,4096]{2,1,0:T(8,128)(2,1)}, u32[]{:S(2)}) copy-start(bf16[2,8,4096]{2,1,0:T(8,128)(2,1)} %param.7) | copy-start | bytes 393220
  7.4 9.0 %copy-start.2 = (s32[2,2]{1,0:T(2,128)S(1)}, s32[2,2]{1,0:T(2,128)}, u32[]{:S(2)}) copy-start(s32[2,2]{1,0:T(2,128)} %param.8) | copy-start | bytes 52
  16.2 0.7 copy-start.3
  16.2 97.3 %all-reduce.7.cloned.1.call-start = ((), (), s32[]{:S(2)}) async-start(), calls=%async_computation | async-start | bytes 524288 | tf_op jit(solution)/shard_map/psum | solution.py:87
Sparse Core Ops, SparseCore 0:
  16.4 37.4 all-reduce.8
  81.5 31.9 all-reduce.6
where the time goes:
time: 122 us
  waiting for transfers between devices  39.5 us (32%)
  blocking collectives  33.9 us (28%)
  matrix products  22 us (18%)
  between operations  14.2 us (12%)
  local copies, waits for them, and re-layouts  8.61 us (7%)
  other arithmetic  3.71 us (3%)
    psum x1, waiting for transfers between devices, local(): summed_heads = lax.psum(projected, 'gy')  32.2 us
    unnamed x1, blocking collectives  20.8 us
    all_gather x1, blocking collectives, local(): lax.all_gather(attended, 'gx', axis=1, tiled=True)  13.1 us
    dot_general x1, matrix products, local(): jnp.einsum('mrd,dc->mrc', normed, w_query, preferred_element_type=jnp.flo...  8.81 us
    dot_general x1, matrix products, local(): jnp.einsum('mrc,cd->mrd', lax.all_gather(attended, 'gx', axis=1, tiled=Tr...  8.75 us
    unnamed x3, waiting for transfers between devices  7.38 us
    slice x1, local copies, waits for them, and re-layouts, attend(): keys = cache[:, :, :, :, 0, :]  6.95 us
  transfers between devices with their start and end apart: 2, of which 2 were waited for; matrix products, arithmetic and copies ran while one was open for 7% of the time, Pallas kernels for 0%

commit v1 on v0

--- a/solution.py
+++ b/solution.py
@@ -5,6 +5,14 @@
 
 MODEL_WIDTH = 16384
 HEAD_SIZE = 128
+
+
+def add_in_pairs(x, mesh_axis):
+    devices, total = (lax.axis_size(mesh_axis), x)
+    for far in [1 << k for k in range(devices.bit_length() - 1)]:
+        pairs = [(i, i ^ far) for i in range(devices)]
+        total = total + lax.ppermute(total, mesh_axis, pairs)
+    return total
 
 
 def rotate(vectors, positions):
@@ -84,7 +92,7 @@
         w_out,
         preferred_element_type=jnp.float32,
     )
-    summed_heads = lax.psum(projected, "gy")
+    summed_heads = add_in_pairs(projected, "gy")
     return (x_full + summed_heads).astype(jnp.bfloat16)
 
 

time: 122 us -> 98.6 us (0.81)
  waiting for transfers between devices: 39.5 us -> 15.9 us
  starting transfers between devices: 0.04 us -> 1.52 us
    psum x1 -> x0, waiting for transfers between devices: 32.2 us -> none  [local(): summed_heads = lax.psum(projected, 'gy')]
    ppermute x0 -> x2, waiting for transfers between devices: none -> 8.44 us  [add_in_pairs(): total = total + lax.ppermute(total, mesh_axis, pairs)]
    ppermute x0 -> x2, starting transfers between devices: none -> 1.52 us  [add_in_pairs(): total = total + lax.ppermute(total, mesh_axis, pairs)]
    unnamed x3 -> x2, waiting for transfers between devices: 7.38 us -> 7.49 us
  transfers between devices with their start and end apart: 2 -> 3, of which waited for: 2 -> 3; matrix products, arithmetic and copies ran while one was open for 7% -> 9% of each run, Pallas kernels for 0% -> 0%
where the time goes in v1:
time: 98.6 us; the launch traced here: 98.2 us
  blocking collectives  33.9 us (34%)
  matrix products  21.2 us (22%)
  waiting for transfers between devices  15.9 us (16%)
  between operations  14.2 us (14%)
  local copies, waits for them, and re-layouts  8.62 us (9%)
  other arithmetic  2.81 us (3%)
  starting transfers between devices  1.52 us (2%)
    unnamed x1, blocking collectives  20.8 us
    all_gather x1, blocking collectives, local(): lax.all_gather(attended, 'gx', axis=1, tiled=True)  13.1 us
    dot_general x1, matrix products, local(): jnp.einsum('mrd,dc->mrc', normed, w_query, preferred_element_type=jnp.flo...  8.81 us
    ppermute x2, waiting for transfers between devices, add_in_pairs(): total = total + lax.ppermute(total, mesh_axis, pairs)  8.44 us
    dot_general x1, matrix products, local(): jnp.einsum('mrc,cd->mrd', lax.all_gather(attended, 'gx', axis=1, tiled=Tr...  8.05 us
    unnamed x2, waiting for transfers between devices  7.49 us
    slice x1, local copies, waits for them, and re-layouts, attend(): keys = cache[:, :, :, :, 0, :]  6.95 us
    dot_general x1, matrix products, attend(): jnp.einsum('mrkgd,mrskd->mrkgs', rotated_query, keys, preferred_element_t...  2.1 us
  transfers between devices with their start and end apart: 3, of which 3 were waited for; matrix products, arithmetic and copies ran while one was open for 9% of the time, Pallas kernels for 0%

profile of v1, /device:TPU:0, one launch (start us, length us, event | category | flops | bytes accessed | tf_op | source)
XLA Modules:
  0.0 98.2 jit_solution(3307782136391709353)
XLA Ops:
  6.5 0.8 convert_element_type.46
  7.4 8.8 %fusion.2 = f32[2,8,2048]{2,1,0:T(8,128)} fusion(bf16[4096,2048]{1,0:T(8,128)(2,1)} %param.10, bf16[2,8,4096]{2,1,0:T(8,128)(2,1)} %param.7, f32[4096]{0:T(1024)S(1)} %convert_element_type.46), kind=kOutput, calls=%fused_computation.2 | convolution fusion | flops 268632064 | bytes 17055744 | tf_op jit(solution)/shard_map/mrd,dc->mrc/dot_general | solution.py:79
  16.3 0.1 fusion.13
  16.4 0.1 iota_compare_fusion
  16.5 0.4 fusion.9
  16.9 0.7 dynamic-slice
  18.2 0.1 multiply_cosine_fusion.1
  18.4 20.8 %all-reduce.3 = (f32[2,8]{1,0:T(2,128)S(1)}, f32[2,8,1,256]{3,1,0,2:T(8,128)S(1)}) all-reduce(f32[2,8]{1,0:T(2,128)S(1)} %fusion.13, f32[2,8,1,256]{3,1,0,2:T(8,128)S(1)} %fusion.9), channel_id=3, replica_groups=mesh['groups'=2,'gx'=4,'gy'=4] {'gx'}, use_global_device_ids=true, to_apply=%region_2.0.clone | all-reduce | flops 4112 | bytes 32896
  39.2 0.1 dynamic-slice_multiply_fusion
  39.3 0.1 fusion.29
  39.4 7.0 %fusion.35 = (bf16[2,2,1024,1,1,128]{5,4,3,2,1,0:T(2,128)(2,1)}, bf16[2,2,1024,1,1,128]{5,4,3,2,1,0:T(2,128)(2,1)}) fusion(bf16[2,2,1024,1,2,128]{5,4,3,2,1,0:T(2,128)(2,1)} %param.13), kind=kLoop, calls=%fused_computation.55 | loop fusion | bytes 4194304 | tf_op jit(solution)/shard_map/slice | solution.py:46
  46.4 7.5 %all-reduce.6.cloned.1.call-done = f32[2,8,2048]{2,1,0:T(8,128)} async-done(((f32[2,8,2048]{2,1,0:T(8,128)}), f32[2,8,2048]{2,1,0:T(8,128)}) %all-reduce.6.cloned.1.call-update) | async-done | bytes 131088
  53.9 0.9 constant_dynamic-slice_fusion
  54.9 0.1 subtract_convert_fusion
  55.0 0.2 multiply_reduce_fusion
  55.2 2.1 %fusion.36 = (f32[2,2,16]{2,1,0:T(2,128)S(1)}, f32[2,2,16,1024]{3,2,1,0:T(8,128)S(1)}) fusion(bf16[2,2,1024,1,1,128]{5,4,3,2,1,0:T(2,128)(2,1)} %get-tuple-element.9, bf16[2,2,16,64]{3,2,1,0:T(8,128)(2,1)S(1)} %bitcast.38, bf16[2,2,16,64]{3,2,1,0:T(8,128)(2,1)S(1)} %bitcast.37, pred[2,2,1024]{2,1,0:T(4,128)(4,1)S(1)} %iota_compare_fusion), kind=kOutput, calls=%fused_computation.56 | convolution fusion | flops 17006528 | bytes 1331456 | tf_op jit(solution)/shard_map/mrkgd,mrskd->mrkgs/dot_general | solution.py:49
  57.3 0.2 fusion.15
  57.5 1.9 %fusion.8 = bf16[2,2,16,128]{3,2,1,0:T(8,128)(2,1)S(1)} fusion(bf16[2,2,1024,1,1,128]{5,4,3,2,1,0:T(2,128)(2,1)} %get-tuple-element.10, f32[2,2,16,1024]{3,2,1,0:T(8,128)S(1)} %get-tuple-element.18, f32[2,2,16]{2,1,0:T(2,128)S(1)} %multiply_maximum_fusion, f32[2,2,16]{2,1,0:T(2,128)S(1)} %get-tuple-element.7, f32[2,2,128]{2,1,0:T(2,128)S(1)} %slice_bitcast_fusion, ...), kind=kOutput, calls=%fused_computation.10 | convolution fusion | flops 16941056 | bytes 1329920 | tf_op jit(solution)/shard_map/mrkgs,mrskd->mrkgd/dot_general | solution.py:61
  59.5 13.1 %all_gather.3 = bf16[2,8,2048]{2,0,1:T(2,128)(2,1)S(1)} all-gather(bf16[2,2,2048]{2,0,1:T(2,128)(2,1)S(1)} %copy.12), channel_id=1, replica_groups=mesh['groups'=2,'gx'=4,'gy'=4] {'gx'}, dimensions={1}, use_global_device_ids=true | all-gather | bytes 81920 | tf_op jit(solution)/shard_map/all_gather | solution.py:91
  72.6 8.0 %fusion = f32[2,8,4096]{2,1,0:T(8,128)S(1)} fusion(bf16[2048,4096]{1,0:T(8,128)(2,1)} %param.12, bf16[2,8,2048]{2,0,1:T(2,128)(2,1)S(1)} %all_gather.3), kind=kOutput, calls=%fused_computation | convolution fusion | flops 268435456 | bytes 17104896 | tf_op jit(solution)/shard_map/mrc,cd->mrd/dot_general | solution.py:89
  80.7 1.5 %collective-permute-done = f32[2,8,4096]{2,1,0:T(8,128)S(1)} collective-permute-done((f32[2,8,4096]{2,1,0:T(8,128)S(1)}, f32[2,8,4096]{2,1,0:T(8,128)S(1)}, u32[]{:S(2)}, u32[]{:S(2)}) %collective-permute-start) | collective-permute-done | bytes 262176 | tf_op jit(solution)/shard_map/ppermute | solution.py:14
  82.2 1.5 %collective-permute-start.1 = (f32[2,8,4096]{2,1,0:T(8,128)S(1)}, f32[2,8,4096]{2,1,0:T(8,128)S(1)}, u32[]{:S(2)}, u32[]{:S(2)}) collective-permute-start(f32[2,8,4096]{2,1,0:T(8,128)S(1)} %add.42), channel_id=1, source_target_pairs={{0,2},{1,3},{2,0},{3,1},{4,6},{5,7},{6,4},{7,5},{8,10},{9,11},{10,... | collective-permute-start | bytes 786440 | tf_op jit(solution)/shard_map/ppermute | solution.py:14
  83.7 6.9 %collective-permute-done.1 = f32[2,8,4096]{2,1,0:T(8,128)S(1)} collective-permute-done((f32[2,8,4096]{2,1,0:T(8,128)S(1)}, f32[2,8,4096]{2,1,0:T(8,128)S(1)}, u32[]{:S(2)}, u32[]{:S(2)}) %collective-permute-start.1) | collective-permute-done | bytes 262176 | tf_op jit(solution)/shard_map/ppermute | solution.py:14
  90.6 0.7 fusion.14
  (23 shorter events, 0.4 us)
Async XLA Ops:
  6.5 9.9 %copy-start = (bf16[4096,1,256]{2,0,1:T(8,128)(2,1)S(1)}, bf16[4096,1,256]{2,0,1:T(8,128)(2,1)}, u32[]{:S(2)}) copy-start(bf16[4096,1,256]{2,0,1:T(8,128)(2,1)} %param.11) | copy-start | bytes 6291460
  6.5 47.4 %all-reduce.6.cloned.1.call-start = ((), (), s32[]{:S(2)}) async-start(), calls=%async_computation | async-start | bytes 262144
  7.4 8.9 %copy-start.1 = (bf16[2,8,4096]{2,1,0:T(8,128)(2,1)S(1)}, bf16[2,8,4096]{2,1,0:T(8,128)(2,1)}, u32[]{:S(2)}) copy-start(bf16[2,8,4096]{2,1,0:T(8,128)(2,1)} %param.7) | copy-start | bytes 393220
  7.4 9.0 %copy-start.2 = (s32[2,2]{1,0:T(2,128)S(1)}, s32[2,2]{1,0:T(2,128)}, u32[]{:S(2)}) copy-start(s32[2,2]{1,0:T(2,128)} %param.8) | copy-start | bytes 52
  16.2 0.7 copy-start.3
  80.7 1.5 %collective-permute-start = (f32[2,8,4096]{2,1,0:T(8,128)S(1)}, f32[2,8,4096]{2,1,0:T(8,128)S(1)}, u32[]{:S(2)}, u32[]{:S(2)}) collective-permute-start(f32[2,8,4096]{2,1,0:T(8,128)S(1)} %fusion), channel_id=1, source_target_pairs={{0,1},{1,0},{2,3},{3,2},{4,5},{5,4},{6,7},{7,6},{8,9},{9,8},{10,11... | collective-permute-start | bytes 786440 | tf_op jit(solution)/shard_map/ppermute | solution.py:14
  82.2 8.4 %collective-permute-start.1 = (f32[2,8,4096]{2,1,0:T(8,128)S(1)}, f32[2,8,4096]{2,1,0:T(8,128)S(1)}, u32[]{:S(2)}, u32[]{:S(2)}) collective-permute-start(f32[2,8,4096]{2,1,0:T(8,128)S(1)} %add.42), channel_id=1, source_target_pairs={{0,2},{1,3},{2,0},{3,1},{4,6},{5,7},{6,4},{7,5},{8,10},{9,11},{10,... | collective-permute-start | bytes 786440 | tf_op jit(solution)/shard_map/ppermute | solution.py:14
Sparse Core Ops, SparseCore 0:
  16.4 37.5 all-reduce.5
